TPU v7x, 32 devices: a whole 2x2x4 slice. The times are simulated.
32 devices in a mesh: seq: 16 (over z, y, x), blk: 2 (over core).
Axes of the slice: x: 2, y: 2, z: 4, core: 2. Of those that a mesh axis runs over, the one named last changes fastest.
Arguments:
- query: bfloat16 [2048, 5120], P(('blk', 'seq')), may hold values from -139 to 139
- keys: bfloat16 [2048, 5120], P(('blk', 'seq')), may hold values from -4.5 to 4.5
- values: bfloat16 [2048, 5120], P(('blk', 'seq')), may hold values from -6 to 6
Outputs:
- attended: bfloat16 [2048, 5120], P(('blk', 'seq'))
All inputs are finite; a program needn't handle non-finite values.
Results may differ from a plain program's by a relative error of at most 0.008.
Values may be sent and summed in bfloat16 or wider, within the bound.
No kernel may reach another device: no remote copies, remote signals or barrier semaphores. Data moves between devices by JAX's collectives and lax.ppermute only.
A program may use at most 64 MiB of HBM per device.

v0:
```python
import jax
import jax.numpy as jnp
from jax import lax
from jax.sharding import PartitionSpec as P

HEADS = 40


def partner(value, axis, bit):
    mask = 2**bit
    pairs = [(source, source ^ mask) for source in range(lax.axis_size(axis))]
    return lax.ppermute(value, axis, pairs)


def partial_block(q_rows, k_tile, v_tile):
    scores = lax.dot_general(
        q_rows, k_tile, (((1,), (1,)), ((), ())), preferred_element_type=jnp.float32
    ) * q_rows.shape[1] ** (-0.5)
    peak = jnp.max(scores, axis=1)
    expo = jnp.exp(scores - peak[:, None])
    totals = jnp.sum(expo, axis=1)
    summed = jnp.dot(expo.astype(jnp.bfloat16), v_tile, preferred_element_type=jnp.float32)
    return (peak, totals, summed)


def combine_parts(left, right):
    peak = jnp.maximum(left[0], right[0])
    scale_left = jnp.exp(left[0] - peak)
    scale_right = jnp.exp(right[0] - peak)
    totals = scale_left * left[1] + scale_right * right[1]
    summed = scale_left[:, None] * left[2] + scale_right[:, None] * right[2]
    return (peak, totals, summed)


def attend_rows(q_rows, first_k, first_v, second_k, second_v):
    state = partial_block(q_rows, first_k, first_v)
    state = combine_parts(state, partial_block(q_rows, second_k, second_v))
    return (state[2] / state[1][:, None]).astype(jnp.bfloat16)


def attend_item(args):
    q_head, first_k, first_v, second_k, second_v = args
    length, width = q_head.shape
    rows = min(512, length)

    def block(q_rows):
        return attend_rows(q_rows, first_k, first_v, second_k, second_v)

    return lax.map(block, q_head.reshape(length // rows, rows, width)).reshape(length, width)


def items_first(array):
    return jnp.transpose(array.reshape(array.shape[0], array.shape[2], array.shape[3]), (1, 0, 2))


def attend_items(pieces):
    q_group, k_group, v_group = pieces
    q_heads = items_first(q_group)
    k_heads = items_first(k_group)
    v_heads = items_first(v_group)
    stacked = jnp.stack([k_heads, v_heads])
    other = partner(stacked, "blk", 0)
    tiles = (q_heads, k_heads, v_heads, other[0], other[1])
    outcome = lax.map(attend_item, tiles)
    count, length, width = outcome.shape
    outcome = jnp.transpose(outcome, (1, 0, 2)).reshape(length, 1, count, width)
    return lax.all_to_all(outcome, "seq", split_axis=0, concat_axis=1, tiled=True)


def on_device(query, keys, values):
    groups = lax.axis_size("seq")
    width = query.shape[1] // HEADS
    tok_rows = query.shape[0]
    key_source, value_source = (keys, values)
    per_dev = (HEADS + groups - 1) // groups
    slots_all = per_dev * groups

    def split_heads(array):
        count_rows = array.shape[0]
        shaped = array.reshape(count_rows, HEADS, width)
        shaped = jnp.pad(shaped, ((0, 0), (0, slots_all - HEADS), (0, 0)))
        return shaped.reshape(count_rows, groups, per_dev, width)

    result = attend_items(
        (
            lax.all_to_all(split_heads(query), "seq", split_axis=1, concat_axis=0, tiled=True),
            lax.all_to_all(split_heads(key_source), "seq", split_axis=1, concat_axis=0, tiled=True),
            lax.all_to_all(
                split_heads(value_source), "seq", split_axis=1, concat_axis=0, tiled=True
            ),
        )
    )
    result = result.reshape(tok_rows, slots_all, width)[:, :HEADS]
    return result.reshape(tok_rows, HEADS * width)


def solution(mesh):
    placed = (P(("blk", "seq"), None), P(("blk", "seq"), None), P(("blk", "seq"), None))
    return jax.shard_map(
        on_device, mesh=mesh, in_specs=placed, out_specs=P(("blk", "seq"), None), check_vma=False
    )
```

profile of v0, /device:TPU:0, one launch (start us, length us, event | category | flops | bytes accessed | tf_op | source)
XLA Modules:
  0.0 155.3 jit_solution(6471587082868300585)
XLA Ops:
  0.0 1.1 copy-done
  1.3 1.0 pad.11.clone
  2.2 8.3 %all-to-all-start.1 = ((bf16[64,16,3,128]{3,0,2,1:T(8,128)(2,1)}), bf16[64,16,3,128]{3,0,2,1:T(8,128)(2,1)S(1)}, u32[]{:S(2)}, u32[]{:S(2)}) async-start(bf16[64,16,3,128]{3,0,2,1:T(8,128)(2,1)} %bitcast.13), calls=%async_computation.1 | async-start | bytes 1572864 | tf_op jit(solution)/shard_map/all_to_all | solution.py:87
  10.8 1.0 pad.12.clone
  11.8 18.5 %all-to-all-done.1 = bf16[64,16,3,128]{3,0,2,1:T(8,128)(2,1)S(1)} async-done(((bf16[64,16,3,128]{3,0,2,1:T(8,128)(2,1)}), bf16[64,16,3,128]{3,0,2,1:T(8,128)(2,1)S(1)}, u32[]{:S(2)}, u32[]{:S(2)}) %all-to-all-start.1) | async-done | bytes 786464 | tf_op jit(solution)/shard_map/all_to_all | solution.py:87
  30.3 5.0 %all-to-all-start.2 = ((bf16[64,16,3,128]{3,0,2,1:T(8,128)(2,1)}), bf16[64,16,3,128]{3,0,2,1:T(8,128)(2,1)S(1)}, u32[]{:S(2)}, u32[]{:S(2)}) async-start(bf16[64,16,3,128]{3,0,2,1:T(8,128)(2,1)} %bitcast.18), calls=%async_computation.2 | async-start | bytes 1572864 | tf_op jit(solution)/shard_map/all_to_all | solution.py:88
  35.3 18.6 %all-to-all-done.2 = bf16[64,16,3,128]{3,0,2,1:T(8,128)(2,1)S(1)} async-done(((bf16[64,16,3,128]{3,0,2,1:T(8,128)(2,1)}), bf16[64,16,3,128]{3,0,2,1:T(8,128)(2,1)S(1)}, u32[]{:S(2)}, u32[]{:S(2)}) %all-to-all-start.2) | async-done | bytes 786464 | tf_op jit(solution)/shard_map/all_to_all | solution.py:88
  53.9 0.9 copy-done.2
  54.8 1.3 copy.18
  56.0 1.3 pad_maximum_fusion
  57.5 1.0 pad.10.clone
  58.5 5.0 %all-to-all-start = ((bf16[64,16,3,128]{3,0,2,1:T(8,128)(2,1)}), bf16[64,16,3,128]{3,0,2,1:T(8,128)(2,1)S(1)}, u32[]{:S(2)}, u32[]{:S(2)}) async-start(bf16[64,16,3,128]{3,0,2,1:T(8,128)(2,1)} %bitcast.121), calls=%async_computation | async-start | bytes 1572864 | tf_op jit(solution)/shard_map/all_to_all | solution.py:86
  63.4 20.1 %all-to-all-done = bf16[64,16,3,128]{3,0,2,1:T(8,128)(2,1)S(1)} async-done(((bf16[64,16,3,128]{3,0,2,1:T(8,128)(2,1)}), bf16[64,16,3,128]{3,0,2,1:T(8,128)(2,1)S(1)}, u32[]{:S(2)}, u32[]{:S(2)}) %all-to-all-start) | async-done | bytes 786464 | tf_op jit(solution)/shard_map/all_to_all | solution.py:86
  83.5 0.9 copy.14
  84.5 2.6 %slice_bitcast_fusion = (bf16[3,1024,128]{2,1,0:T(8,128)(2,1)}, bf16[3,1024,128]{2,1,0:T(8,128)(2,1)}) fusion(bf16[2,3,1024,128]{3,2,1,0:T(8,128)(2,1)} %collective-permute-done), kind=kLoop, calls=%fused_computation.42 | loop fusion | bytes 3145728 | tf_op jit(solution)/shard_map/squeeze | solution.py:63
  87.1 34.5 %while.21 = (s32[]{:T(128)}, bf16[3,1024,128]{2,1,0:T(8,128)(2,1)}, bf16[3,1024,128]{2,1,0:T(8,128)(2,1)}, bf16[3,1024,128]{2,1,0:T(8,128)(2,1)S(1)}, bf16[3,102...) while((s32[]{:T(128)}, bf16[3,1024,128]{2,1,0:T(8,128)(2,1)}, ...), condition=%wide.region_7.8_spmd, body=%wide.region_0.7_spmd.sunk | while | flops 545588224 | bytes 18780980 | solution.py:64
  87.1 1.0 dynamic-slice_bitcast_fusion.6
  88.1 1.7 %dynamic-slice_bitcast_fusion.7 = (bf16[1024,128]{1,0:T(8,128)(2,1)}, bf16[1024,128]{1,0:T(8,128)(2,1)S(1)}) fusion(bf16[3,1024,128]{2,1,0:T(8,128)(2,1)} %get-tuple-element.302, s32[]{:T(128)} %get-tuple-element.286, bf16[3,1024,128]{2,1,0:T(8,128)(2,1)S(1)} %get-tuple-element.300), kind=kLoop, calls=%fused_computation.35.clone.1 | loop fusion | bytes 1048580 | tf_op jit(solution)/shard_map/while/body/jit(dynamic_index_in_dim)/squeeze | solution.py:64
  89.8 1.0 constant_dynamic-slice_fusion.2
  90.8 7.1 %while.22 = (s32[]{:T(128)}, bf16[2,512,128]{2,1,0:T(8,128)(2,1)S(1)}, bf16[2,512,128]{2,1,0:T(8,128)(2,1)S(1)}, bf16[1024,128]{1,0:T(8,128)(2,1)S(1)}, bf16[102...) while((s32[]{:T(128)}, ...), condition=%wide.region_6.6_spmd, body=%wide.region_1.5_spmd.sunk | while | flops 545588224 | bytes 15634557 | solution.py:49
  90.8 0.5 multiply_reduce_fusion.4
  91.3 0.5 multiply_reduce_fusion.5
  91.8 1.0 fusion.50
  92.8 0.5 convolution_multiply_fusion.3
  93.7 0.6 fusion.51
  94.3 0.5 multiply_reduce_fusion.4
  94.9 0.5 multiply_reduce_fusion.5
  95.4 1.0 fusion.50
  96.4 0.5 convolution_multiply_fusion.3
  97.3 0.6 fusion.51
  97.9 0.7 bitcast_dynamic-update-slice_fusion.2
  98.6 1.0 dynamic-slice_bitcast_fusion.6
  99.6 1.7 %dynamic-slice_bitcast_fusion.7 = (bf16[1024,128]{1,0:T(8,128)(2,1)}, bf16[1024,128]{1,0:T(8,128)(2,1)S(1)}) fusion(bf16[3,1024,128]{2,1,0:T(8,128)(2,1)} %get-tuple-element.302, s32[]{:T(128)} %get-tuple-element.286, bf16[3,1024,128]{2,1,0:T(8,128)(2,1)S(1)} %get-tuple-element.300), kind=kLoop, calls=%fused_computation.35.clone.1 | loop fusion | bytes 1048580 | tf_op jit(solution)/shard_map/while/body/jit(dynamic_index_in_dim)/squeeze | solution.py:64
  101.3 1.0 constant_dynamic-slice_fusion.2
  102.3 7.1 %while.22 = (s32[]{:T(128)}, bf16[2,512,128]{2,1,0:T(8,128)(2,1)S(1)}, bf16[2,512,128]{2,1,0:T(8,128)(2,1)S(1)}, bf16[1024,128]{1,0:T(8,128)(2,1)S(1)}, bf16[102...) while((s32[]{:T(128)}, ...), condition=%wide.region_6.6_spmd, body=%wide.region_1.5_spmd.sunk | while | flops 545588224 | bytes 15634557 | solution.py:49
  102.3 0.5 multiply_reduce_fusion.4
  102.8 0.5 multiply_reduce_fusion.5
  103.3 1.0 fusion.50
  104.3 0.5 convolution_multiply_fusion.3
  105.2 0.6 fusion.51
  105.8 0.5 multiply_reduce_fusion.4
  106.3 0.5 multiply_reduce_fusion.5
  106.9 1.0 fusion.50
  107.8 0.5 convolution_multiply_fusion.3
  108.8 0.6 fusion.51
  109.4 0.7 bitcast_dynamic-update-slice_fusion.2
  110.1 1.0 dynamic-slice_bitcast_fusion.6
  111.1 1.7 %dynamic-slice_bitcast_fusion.7 = (bf16[1024,128]{1,0:T(8,128)(2,1)}, bf16[1024,128]{1,0:T(8,128)(2,1)S(1)}) fusion(bf16[3,1024,128]{2,1,0:T(8,128)(2,1)} %get-tuple-element.302, s32[]{:T(128)} %get-tuple-element.286, bf16[3,1024,128]{2,1,0:T(8,128)(2,1)S(1)} %get-tuple-element.300), kind=kLoop, calls=%fused_computation.35.clone.1 | loop fusion | bytes 1048580 | tf_op jit(solution)/shard_map/while/body/jit(dynamic_index_in_dim)/squeeze | solution.py:64
  112.8 1.0 constant_dynamic-slice_fusion.2
  113.8 7.1 %while.22 = (s32[]{:T(128)}, bf16[2,512,128]{2,1,0:T(8,128)(2,1)S(1)}, bf16[2,512,128]{2,1,0:T(8,128)(2,1)S(1)}, bf16[1024,128]{1,0:T(8,128)(2,1)S(1)}, bf16[102...) while((s32[]{:T(128)}, ...), condition=%wide.region_6.6_spmd, body=%wide.region_1.5_spmd.sunk | while | flops 545588224 | bytes 15634557 | solution.py:49
  113.8 0.5 multiply_reduce_fusion.4
  114.3 0.5 multiply_reduce_fusion.5
  114.8 1.0 fusion.50
  115.8 0.5 convolution_multiply_fusion.3
  116.7 0.6 fusion.51
  117.3 0.5 multiply_reduce_fusion.4
  117.8 0.5 multiply_reduce_fusion.5
  118.4 1.0 fusion.50
  119.3 0.5 convolution_multiply_fusion.3
  120.3 0.6 fusion.51
  120.9 0.7 bitcast_dynamic-update-slice_fusion.2
  121.6 1.8 %copy.35 = bf16[3,1024,128]{2,0,1:T(4,128)(2,1)S(1)} copy(bf16[3,1024,128]{2,1,0:T(8,128)(2,1)} %get-tuple-element.79) | data formatting | bytes 1572864 | tf_op jit(solution)/shard_map/while | solution.py:64
  123.4 30.8 %all_to_all.60 = bf16[1024,1,3,128]{3,2,1,0:T(4,128)(2,1)S(1)} all-to-all(bf16[1024,1,3,128]{3,2,1,0:T(4,128)(2,1)S(1)} %bitcast.116), channel_id=1, replica_groups=mesh['seq'=16,'blk'=2] {'seq'}, dimensions={0} | all-to-all | bytes 1572864 | tf_op jit(solution)/shard_map/all_to_all | solution.py:67
  154.4 0.9 copy_bitcast_fusion.1
  (36 shorter events, 3.2 us)
Async XLA Ops:
  0.0 1.1 copy-start
  0.0 10.6 %copy-start.3 = (bf16[64,5120]{1,0:T(8,128)(2,1)S(1)}, bf16[64,5120]{1,0:T(8,128)(2,1)}, u32[]{:S(2)}) copy-start(bf16[64,5120]{1,0:T(8,128)(2,1)} %param.9) | copy-start | bytes 1966084
  2.2 28.0 %all-to-all-start.1 = ((bf16[64,16,3,128]{3,0,2,1:T(8,128)(2,1)}), bf16[64,16,3,128]{3,0,2,1:T(8,128)(2,1)S(1)}, u32[]{:S(2)}, u32[]{:S(2)}) async-start(bf16[64,16,3,128]{3,0,2,1:T(8,128)(2,1)} %bitcast.13), calls=%async_computation.1 | async-start | bytes 1572864 | tf_op jit(solution)/shard_map/all_to_all | solution.py:87
  30.3 23.6 %all-to-all-start.2 = ((bf16[64,16,3,128]{3,0,2,1:T(8,128)(2,1)}), bf16[64,16,3,128]{3,0,2,1:T(8,128)(2,1)S(1)}, u32[]{:S(2)}, u32[]{:S(2)}) async-start(bf16[64,16,3,128]{3,0,2,1:T(8,128)(2,1)} %bitcast.18), calls=%async_computation.2 | async-start | bytes 1572864 | tf_op jit(solution)/shard_map/all_to_all | solution.py:88
  53.9 0.9 copy-start.2
  54.8 2.6 %copy-start.4 = (bf16[64,5120]{1,0:T(8,128)(2,1)S(1)}, bf16[64,5120]{1,0:T(8,128)(2,1)}, u32[]{:S(2)}) copy-start(bf16[64,5120]{1,0:T(8,128)(2,1)} %param.7) | copy-start | bytes 1966084
  57.3 27.2 %collective-permute-start = (bf16[2,3,1024,128]{3,2,1,0:T(8,128)(2,1)}, bf16[2,3,1024,128]{3,2,1,0:T(8,128)(2,1)}, u32[]{:S(2)}, u32[]{:S(2)}) collective-permute-start(bf16[2,3,1024,128]{3,2,1,0:T(8,128)(2,1)} %pad_maximum_fusion), channel_id=1, source_target_pairs={{0,1},{1,0},{2,3},{3,2},{4,5},{5,4},{6,7},{7,6},{8,9},{9,8},{10,11... | collective-permute-start | bytes 4718600 | tf_op jit(solution)/shard_map/ppermute | solution.py:12
  58.5 25.1 %all-to-all-start = ((bf16[64,16,3,128]{3,0,2,1:T(8,128)(2,1)}), bf16[64,16,3,128]{3,0,2,1:T(8,128)(2,1)S(1)}, u32[]{:S(2)}, u32[]{:S(2)}) async-start(bf16[64,16,3,128]{3,0,2,1:T(8,128)(2,1)} %bitcast.121), calls=%async_computation | async-start | bytes 1572864 | tf_op jit(solution)/shard_map/all_to_all | solution.py:86
  92.8 1.0 copy-start.1
  96.3 1.0 copy-start.1
  104.3 1.0 copy-start.1
  107.8 1.0 copy-start.1
  115.8 1.0 copy-start.1
  119.3 1.0 copy-start.1
where the time goes:
time: 156 us; the launch traced here: 155 us
  waiting for transfers between devices  57.1 us (37%)
  blocking collectives  30.8 us (20%)
  local copies, waits for them, and re-layouts  28.7 us (18%)
  starting transfers between devices  18.2 us (12%)
  matrix products  12.9 us (8%)
  other arithmetic  7.11 us (5%)
    all_to_all x1, blocking collectives, attend_items(): lax.all_to_all(outcome, 'seq', split_axis=0, concat_axis=1, tiled=True)  30.8 us
    all_to_all x1, waiting for transfers between devices, on_device(): lax.all_to_all(split_heads(query), 'seq', split_axis=1, concat_axis=0, ti...  20.1 us
    all_to_all x1, waiting for transfers between devices, on_device(): lax.all_to_all(split_heads(value_source), 'seq', split_axis=1, concat_axi...  18.6 us
    all_to_all x1, waiting for transfers between devices, on_device(): lax.all_to_all(split_heads(key_source), 'seq', split_axis=1, concat_axis=...  18.5 us
    all_to_all x1, starting transfers between devices, on_device(): lax.all_to_all(split_heads(key_source), 'seq', split_axis=1, concat_axis=...  8.34 us
    squeeze x6, local copies, waits for them, and re-layouts, attend_items(): outcome = lax.map(attend_item, tiles)  8.03 us
    dot_general x12, matrix products, partial_block(): jnp.dot(expo.astype(jnp.bfloat16), v_tile, preferred_element_type=jnp.flo...  6.67 us
    dot_general x12, matrix products, partial_block(): lax.dot_general(q_rows, k_tile, (((1,), (1,)), ((), ())), preferred_eleme...  6.23 us
  transfers between devices with their start and end apart: 4, of which 3 were waited for; matrix products, arithmetic and copies ran while one was open for 2% of the time, Pallas kernels for 0%

commit v1 on v0

--- a/solution.py
+++ b/solution.py
@@ -83,7 +83,15 @@
 
     result = attend_items(
         (
-            lax.all_to_all(split_heads(query), "seq", split_axis=1, concat_axis=0, tiled=True),
+            jnp.concatenate(
+                lax.all_to_all(
+                    jnp.stack(jnp.split(split_heads(query), lax.axis_size("seq"), axis=1)),
+                    "seq",
+                    0,
+                    0,
+                ),
+                axis=0,
+            ),
             lax.all_to_all(split_heads(key_source), "seq", split_axis=1, concat_axis=0, tiled=True),
             lax.all_to_all(
                 split_heads(value_source), "seq", split_axis=1, concat_axis=0, tiled=True

time: 156 us -> 155 us (level)
  waiting for transfers between devices: 57.1 us -> 47.5 us
  local copies, waits for them, and re-layouts: 28.7 us -> 36.5 us
    unnamed x11 -> x25, local copies, waits for them, and re-layouts: 2.49 us -> 10.8 us
    all_to_all x1, waiting for transfers between devices: 18.5 us -> 13.2 us  [on_device(): lax.all_to_all(split_heads(key_source), 'seq', split_axis=1, concat_axis=...]
    all_to_all x1, waiting for transfers between devices: 18.6 us -> 14.2 us  [on_device(): lax.all_to_all(split_heads(value_source), 'seq', split_axis=1, concat_axi...]
  transfers between devices with their start and end apart: 4 -> 4, of which waited for: 3 -> 3; matrix products, arithmetic and copies ran while one was open for 2% -> 9% of each run, Pallas kernels for 0% -> 0%
where the time goes in v1:
time: 155 us; the launch traced here: 154 us
  waiting for transfers between devices  47.5 us (31%)
  local copies, waits for them, and re-layouts  36.5 us (24%)
  blocking collectives  30.8 us (20%)
  starting transfers between devices  18.4 us (12%)
  matrix products  12.9 us (8%)
  other arithmetic  7.17 us (5%)
    all_to_all x1, blocking collectives, attend_items(): lax.all_to_all(outcome, 'seq', split_axis=0, concat_axis=1, tiled=True)  30.8 us
    all_to_all x1, waiting for transfers between devices, on_device(): lax.all_to_all(jnp.stack(jnp.split(split_heads(query), lax.axis_size('seq...  20.1 us
    all_to_all x1, waiting for transfers between devices, on_device(): lax.all_to_all(split_heads(value_source), 'seq', split_axis=1, concat_axi...  14.2 us
    all_to_all x1, waiting for transfers between devices, on_device(): lax.all_to_all(split_heads(key_source), 'seq', split_axis=1, concat_axis=...  13.2 us
    unnamed x25, local copies, waits for them, and re-layouts  10.8 us
    all_to_all x1, starting transfers between devices, on_device(): lax.all_to_all(split_heads(key_source), 'seq', split_axis=1, concat_axis=...  8.47 us
    squeeze x6, local copies, waits for them, and re-layouts, attend_items(): outcome = lax.map(attend_item, tiles)  8.03 us
    dot_general x12, matrix products, partial_block(): jnp.dot(expo.astype(jnp.bfloat16), v_tile, preferred_element_type=jnp.flo...  6.67 us
  transfers between devices with their start and end apart: 4, of which 3 were waited for; matrix products, arithmetic and copies ran while one was open for 9% of the time, Pallas kernels for 0%

profile of v1, /device:TPU:0, one launch (start us, length us, event | category | flops | bytes accessed | tf_op | source)
XLA Modules:
  0.0 153.7 jit_solution(8396472320951399135)
XLA Ops:
  0.0 1.1 copy-done
  1.3 1.0 pad.11.clone
  2.2 8.5 %all-to-all-start.1 = ((bf16[64,16,3,128]{3,0,2,1:T(8,128)(2,1)}), bf16[64,16,3,128]{3,0,2,1:T(8,128)(2,1)S(1)}, u32[]{:S(2)}, u32[]{:S(2)}) async-start(bf16[64,16,3,128]{3,0,2,1:T(8,128)(2,1)} %bitcast.27), calls=%async_computation.1 | async-start | bytes 1572864 | tf_op jit(solution)/shard_map/all_to_all | solution.py:95
  11.0 0.7 fusion.42
  11.9 1.0 pad.12.clone
  12.8 0.6 fusion.41
  13.5 0.6 fusion.40
  14.1 0.6 fusion.39
  14.7 0.6 fusion.38
  15.3 0.6 fusion.37
  16.0 0.6 fusion.36
  16.6 0.6 fusion.35
  17.2 13.2 %all-to-all-done.1 = bf16[64,16,3,128]{3,0,2,1:T(8,128)(2,1)S(1)} async-done(((bf16[64,16,3,128]{3,0,2,1:T(8,128)(2,1)}), bf16[64,16,3,128]{3,0,2,1:T(8,128)(2,1)S(1)}, u32[]{:S(2)}, u32[]{:S(2)}) %all-to-all-start.1) | async-done | bytes 786464 | tf_op jit(solution)/shard_map/all_to_all | solution.py:95
  30.4 5.0 %all-to-all-start.2 = ((bf16[64,16,3,128]{3,0,2,1:T(8,128)(2,1)}), bf16[64,16,3,128]{3,0,2,1:T(8,128)(2,1)S(1)}, u32[]{:S(2)}, u32[]{:S(2)}) async-start(bf16[64,16,3,128]{3,0,2,1:T(8,128)(2,1)} %bitcast.32), calls=%async_computation.2 | async-start | bytes 1572864 | tf_op jit(solution)/shard_map/all_to_all | solution.py:96
  35.4 0.6 fusion.34
  36.0 0.6 fusion.33
  36.6 0.6 fusion.32
  37.2 0.6 fusion.31
  37.9 0.6 fusion.30
  38.5 0.6 fusion.29
  39.1 0.6 fusion.28
  39.8 14.2 %all-to-all-done.2 = bf16[64,16,3,128]{3,0,2,1:T(8,128)(2,1)S(1)} async-done(((bf16[64,16,3,128]{3,0,2,1:T(8,128)(2,1)}), bf16[64,16,3,128]{3,0,2,1:T(8,128)(2,1)S(1)}, u32[]{:S(2)}, u32[]{:S(2)}) %all-to-all-start.2) | async-done | bytes 786464 | tf_op jit(solution)/shard_map/all_to_all | solution.py:96
  54.1 1.3 pad_maximum_fusion
  55.4 1.4 fusion.27
  56.8 5.0 %all-to-all-start = ((bf16[16,64,1,3,128]{4,1,3,2,0:T(8,128)(2,1)}), bf16[16,64,1,3,128]{4,1,3,2,0:T(8,128)(2,1)S(1)}, u32[]{:S(2)}, u32[]{:S(2)}) async-start(bf16[16,64,1,3,128]{4,1,3,2,0:T(8,128)(2,1)} %fusion.27), calls=%async_computation | async-start | bytes 1572864 | tf_op jit(solution)/shard_map/all_to_all | solution.py:87
  61.8 20.1 %all-to-all-done = bf16[16,64,1,3,128]{4,1,3,2,0:T(8,128)(2,1)S(1)} async-done(((bf16[16,64,1,3,128]{4,1,3,2,0:T(8,128)(2,1)}), bf16[16,64,1,3,128]{4,1,3,2,0:T(8,128)(2,1)S(1)}, u32[]{:S(2)}, u32[]{:S(2)}) %all-to-all-start) | async-done | bytes 786464 | tf_op jit(solution)/shard_map/all_to_all | solution.py:87
  81.9 1.0 copy.69
  82.8 2.6 %slice_bitcast_fusion = (bf16[3,1024,128]{2,1,0:T(8,128)(2,1)}, bf16[3,1024,128]{2,1,0:T(8,128)(2,1)}) fusion(bf16[2,3,1024,128]{3,2,1,0:T(8,128)(2,1)} %collective-permute-done), kind=kLoop, calls=%fused_computation.42 | loop fusion | bytes 3145728 | tf_op jit(solution)/shard_map/squeeze | solution.py:63
  85.5 34.6 %while.21 = (s32[]{:T(128)}, bf16[3,1024,128]{2,1,0:T(8,128)(2,1)}, bf16[3,1024,128]{2,1,0:T(8,128)(2,1)}, bf16[3,1024,128]{2,1,0:T(8,128)(2,1)S(1)}, bf16[3,102...) while((s32[]{:T(128)}, bf16[3,1024,128]{2,1,0:T(8,128)(2,1)}, ...), condition=%wide.region_7.8_spmd, body=%wide.region_0.7_spmd.sunk | while | flops 545588224 | bytes 18780980 | solution.py:64
  85.5 1.0 dynamic-slice_bitcast_fusion.6
  86.4 1.7 %dynamic-slice_bitcast_fusion.7 = (bf16[1024,128]{1,0:T(8,128)(2,1)}, bf16[1024,128]{1,0:T(8,128)(2,1)S(1)}) fusion(bf16[3,1024,128]{2,1,0:T(8,128)(2,1)} %get-tuple-element.302, s32[]{:T(128)} %get-tuple-element.286, bf16[3,1024,128]{2,1,0:T(8,128)(2,1)S(1)} %get-tuple-element.300), kind=kLoop, calls=%fused_computation.35.clone.1 | loop fusion | bytes 1048580 | tf_op jit(solution)/shard_map/while/body/jit(dynamic_index_in_dim)/squeeze | solution.py:64
  88.1 1.0 constant_dynamic-slice_fusion.2
  89.1 7.1 %while.22 = (s32[]{:T(128)}, bf16[2,512,128]{2,1,0:T(8,128)(2,1)S(1)}, bf16[2,512,128]{2,1,0:T(8,128)(2,1)S(1)}, bf16[1024,128]{1,0:T(8,128)(2,1)S(1)}, bf16[102...) while((s32[]{:T(128)}, ...), condition=%wide.region_6.6_spmd, body=%wide.region_1.5_spmd.sunk | while | flops 545588224 | bytes 15634557 | solution.py:49
  90.2 1.0 fusion.66
  91.2 0.5 convolution_multiply_fusion.3
  92.1 0.6 fusion.67
  93.7 1.0 fusion.66
  94.7 0.5 convolution_multiply_fusion.3
  95.7 0.6 fusion.67
  96.3 0.7 bitcast_dynamic-update-slice_fusion.2
  97.0 1.0 dynamic-slice_bitcast_fusion.6
  98.0 1.7 %dynamic-slice_bitcast_fusion.7 = (bf16[1024,128]{1,0:T(8,128)(2,1)}, bf16[1024,128]{1,0:T(8,128)(2,1)S(1)}) fusion(bf16[3,1024,128]{2,1,0:T(8,128)(2,1)} %get-tuple-element.302, s32[]{:T(128)} %get-tuple-element.286, bf16[3,1024,128]{2,1,0:T(8,128)(2,1)S(1)} %get-tuple-element.300), kind=kLoop, calls=%fused_computation.35.clone.1 | loop fusion | bytes 1048580 | tf_op jit(solution)/shard_map/while/body/jit(dynamic_index_in_dim)/squeeze | solution.py:64
  99.7 1.0 constant_dynamic-slice_fusion.2
  100.6 7.1 %while.22 = (s32[]{:T(128)}, bf16[2,512,128]{2,1,0:T(8,128)(2,1)S(1)}, bf16[2,512,128]{2,1,0:T(8,128)(2,1)S(1)}, bf16[1024,128]{1,0:T(8,128)(2,1)S(1)}, bf16[102...) while((s32[]{:T(128)}, ...), condition=%wide.region_6.6_spmd, body=%wide.region_1.5_spmd.sunk | while | flops 545588224 | bytes 15634557 | solution.py:49
  101.7 1.0 fusion.66
  103.6 0.6 fusion.67
  105.2 1.0 fusion.66
  106.2 0.5 convolution_multiply_fusion.3
  107.2 0.6 fusion.67
  107.8 0.7 bitcast_dynamic-update-slice_fusion.2
  108.5 1.0 dynamic-slice_bitcast_fusion.6
  109.5 1.7 %dynamic-slice_bitcast_fusion.7 = (bf16[1024,128]{1,0:T(8,128)(2,1)}, bf16[1024,128]{1,0:T(8,128)(2,1)S(1)}) fusion(bf16[3,1024,128]{2,1,0:T(8,128)(2,1)} %get-tuple-element.302, s32[]{:T(128)} %get-tuple-element.286, bf16[3,1024,128]{2,1,0:T(8,128)(2,1)S(1)} %get-tuple-element.300), kind=kLoop, calls=%fused_computation.35.clone.1 | loop fusion | bytes 1048580 | tf_op jit(solution)/shard_map/while/body/jit(dynamic_index_in_dim)/squeeze | solution.py:64
  111.2 1.0 constant_dynamic-slice_fusion.2
  112.1 7.1 %while.22 = (s32[]{:T(128)}, bf16[2,512,128]{2,1,0:T(8,128)(2,1)S(1)}, bf16[2,512,128]{2,1,0:T(8,128)(2,1)S(1)}, bf16[1024,128]{1,0:T(8,128)(2,1)S(1)}, bf16[102...) while((s32[]{:T(128)}, ...), condition=%wide.region_6.6_spmd, body=%wide.region_1.5_spmd.sunk | while | flops 545588224 | bytes 15634557 | solution.py:49
  113.2 1.0 fusion.66
  114.2 0.5 convolution_multiply_fusion.3
  115.1 0.6 fusion.67
  116.8 1.0 fusion.66
  117.8 0.5 convolution_multiply_fusion.3
  118.7 0.6 fusion.67
  119.3 0.7 bitcast_dynamic-update-slice_fusion.2
  120.0 1.8 %copy.89 = bf16[3,1024,128]{2,0,1:T(4,128)(2,1)S(1)} copy(bf16[3,1024,128]{2,1,0:T(8,128)(2,1)} %get-tuple-element.79) | data formatting | bytes 1572864 | tf_op jit(solution)/shard_map/while | solution.py:64
  121.8 30.8 %all_to_all.50 = bf16[1024,1,3,128]{3,2,1,0:T(4,128)(2,1)S(1)} all-to-all(bf16[1024,1,3,128]{3,2,1,0:T(4,128)(2,1)S(1)} %bitcast.177), channel_id=1, replica_groups=mesh['seq'=16,'blk'=2] {'seq'}, dimensions={0} | all-to-all | bytes 1572864 | tf_op jit(solution)/shard_map/all_to_all | solution.py:67
  152.8 0.9 copy_bitcast_fusion.1
  (52 shorter events, 10.1 us)
Async XLA Ops:
  0.0 1.1 copy-start
  0.0 10.7 %copy-start.3 = (bf16[64,5120]{1,0:T(8,128)(2,1)S(1)}, bf16[64,5120]{1,0:T(8,128)(2,1)}, u32[]{:S(2)}) copy-start(bf16[64,5120]{1,0:T(8,128)(2,1)} %param.7) | copy-start | bytes 1966084
  2.2 9.4 %copy-start.4 = (bf16[64,5120]{1,0:T(8,128)(2,1)S(1)}, bf16[64,5120]{1,0:T(8,128)(2,1)}, u32[]{:S(2)}) copy-start(bf16[64,5120]{1,0:T(8,128)(2,1)} %param.9) | copy-start | bytes 1966084
  2.2 28.2 %all-to-all-start.1 = ((bf16[64,16,3,128]{3,0,2,1:T(8,128)(2,1)}), bf16[64,16,3,128]{3,0,2,1:T(8,128)(2,1)S(1)}, u32[]{:S(2)}, u32[]{:S(2)}) async-start(bf16[64,16,3,128]{3,0,2,1:T(8,128)(2,1)} %bitcast.27), calls=%async_computation.1 | async-start | bytes 1572864 | tf_op jit(solution)/shard_map/all_to_all | solution.py:95
  11.0 28.1 %copy-start.2 = (bf16[64,48,128]{2,0,1:T(8,128)(2,1)}, bf16[64,48,128]{2,0,1:T(8,128)(2,1)S(1)}, u32[]{:S(2)}) copy-start(bf16[64,48,128]{2,0,1:T(8,128)(2,1)S(1)} %pad.10) | copy-start | bytes 2359300
  30.4 23.6 %all-to-all-start.2 = ((bf16[64,16,3,128]{3,0,2,1:T(8,128)(2,1)}), bf16[64,16,3,128]{3,0,2,1:T(8,128)(2,1)S(1)}, u32[]{:S(2)}, u32[]{:S(2)}) async-start(bf16[64,16,3,128]{3,0,2,1:T(8,128)(2,1)} %bitcast.32), calls=%async_computation.2 | async-start | bytes 1572864 | tf_op jit(solution)/shard_map/all_to_all | solution.py:96
  55.4 27.5 %collective-permute-start = (bf16[2,3,1024,128]{3,2,1,0:T(8,128)(2,1)}, bf16[2,3,1024,128]{3,2,1,0:T(8,128)(2,1)}, u32[]{:S(2)}, u32[]{:S(2)}) collective-permute-start(bf16[2,3,1024,128]{3,2,1,0:T(8,128)(2,1)} %pad_maximum_fusion), channel_id=1, source_target_pairs={{0,1},{1,0},{2,3},{3,2},{4,5},{5,4},{6,7},{7,6},{8,9},{9,8},{10,11... | collective-permute-start | bytes 4718600 | tf_op jit(solution)/shard_map/ppermute | solution.py:12
  56.8 25.1 %all-to-all-start = ((bf16[16,64,1,3,128]{4,1,3,2,0:T(8,128)(2,1)}), bf16[16,64,1,3,128]{4,1,3,2,0:T(8,128)(2,1)S(1)}, u32[]{:S(2)}, u32[]{:S(2)}) async-start(bf16[16,64,1,3,128]{4,1,3,2,0:T(8,128)(2,1)} %fusion.27), calls=%async_computation | async-start | bytes 1572864 | tf_op jit(solution)/shard_map/all_to_all | solution.py:87
  91.1 1.0 copy-start.1
  94.7 1.0 copy-start.1
  102.6 1.0 copy-start.1
  106.2 1.0 copy-start.1
  114.2 1.0 copy-start.1
  117.7 1.0 copy-start.1
